TPU v7x, 256 devices: a whole 4x4x8 slice. The times are simulated.
256 devices in a mesh: ep: 16 (over z, core), fsdp: 4 (over x), tp: 4 (over y).
Axes of the slice: x: 4, y: 4, z: 8, core: 2. Of those that a mesh axis runs over, the one named last changes fastest.
Arguments:
- out_grad: bfloat16 [8192, 4096], P(('ep', 'fsdp')), may hold values from -1.5 to 1.5
- routes: int32 [8192, 2], P(('ep', 'fsdp')), may hold values from 0 to 15, all different within a row; in each aligned block of 128 rows (0 to 127, 128 to 255, ...) at most 32 rows name the same one
- chosen_logits: float32 [8192, 2], P(('ep', 'fsdp')), may hold values from -4 to 4
- routed_inputs: bfloat16 [16, 16, 4, 32, 4096], P('ep', None, 'fsdp'), may hold values from -6 to 6
- w_gate: bfloat16 [16, 4096, 1024], P('ep', 'fsdp', 'tp'), may hold values from -0.09375 to 0.09375
- w_up: bfloat16 [16, 4096, 1024], P('ep', 'fsdp', 'tp'), may hold values from -0.09375 to 0.09375
- w_down: bfloat16 [16, 1024, 4096], P('ep', 'tp', 'fsdp'), may hold values from -0.1875 to 0.1875
Outputs:
- input_grad: bfloat16 [8192, 4096], P(('ep', 'fsdp'))
- logit_grad: float32 [8192, 2], P(('ep', 'fsdp'))
- grad_gate: float32 [16, 4096, 1024], P('ep', 'fsdp', 'tp')
- grad_up: float32 [16, 4096, 1024], P('ep', 'fsdp', 'tp')
- grad_down: float32 [16, 1024, 4096], P('ep', 'tp', 'fsdp')
Inputs may be any that keep to these rules, and one draw needn't show every extreme that they name: Each row of routes names 2 different experts. In each token group of 128 consecutive rows no expert is named by more than 32 rows, a bound that some block reaches.
All inputs are finite; a program needn't handle non-finite values.
Results may differ from a plain program's by a relative error of at most 0.015.
Values may be sent and summed in bfloat16 or wider, within the bound.
A program may use at most 128 MiB of HBM per device.

v0:
```python
import jax
import jax.numpy as jnp
from jax import lax
from jax.sharding import PartitionSpec as P


def laid_out(parts, dim):
    shape = list(parts.shape[1:])
    shape[dim] *= parts.shape[0]
    return jnp.moveaxis(parts, 0, dim).reshape(shape)


def gather_together(arrays, axis, dims):
    ravelled = jnp.concatenate([a.reshape(-1) for a in arrays])
    lines, at, outs = lax.all_gather(ravelled, axis), 0, []
    for a, dim in zip(arrays, dims):
        parts = lines[:, at : at + a.size].reshape(-1, *a.shape)
        outs.append(laid_out(parts, dim))
        at += a.size
    return tuple(outs)


def own_rows(product, width, axis):
    whole = product(jnp.int32(0), width * lax.axis_size(axis)).astype(jnp.bfloat16)
    return lax.psum_scatter(whole, axis, scatter_dimension=0, tiled=True).astype(jnp.float32)


def slot_places(routes, experts, capacity):
    flat_routes = routes.reshape(-1)
    onehot = (flat_routes[:, None] == jnp.arange(experts, dtype=jnp.int32)[None, :]).astype(
        jnp.int32
    )
    earlier = (jnp.cumsum(onehot, axis=0) - onehot).astype(jnp.int32)
    position = jnp.sum(earlier * onehot, axis=1).astype(jnp.int32)
    return (flat_routes * capacity + position).astype(jnp.int32)


def weighted_rows(grad_rows, gate_probs):
    scaled = gate_probs[:, :, None] * grad_rows.astype(jnp.float32)[:, None, :]
    return scaled.astype(jnp.bfloat16).reshape(-1, grad_rows.shape[1])


def fill_slots(values, slot_index, total_slots):
    row_total = values.shape[0]
    source = jnp.full((total_slots,), row_total, jnp.int32)
    source = source.at[slot_index].set(jnp.arange(row_total, dtype=jnp.int32))
    padded = jnp.concatenate([values, jnp.zeros((1, values.shape[1]), values.dtype)], axis=0)
    return jnp.take(padded, source, axis=0)


def combine(returned, slot_index, tokens, per_token):
    picked = jnp.take(returned, slot_index, axis=0).astype(jnp.float32)
    return jnp.sum(picked.reshape(tokens, per_token, -1), axis=1).astype(jnp.bfloat16)


def transpose_dot(left, right):
    return lax.dot_general(
        left, right, (((0,), (0,)), ((), ())), preferred_element_type=jnp.float32
    )


def contract_last(left, right):
    return lax.dot_general(
        left, right, (((1,), (1,)), ((), ())), preferred_element_type=jnp.float32
    )


def on_device(out_grad, routes, chosen_logits, routed_inputs, w_gate, w_up, w_down):
    experts = lax.axis_size("ep")
    tp_count = lax.axis_size("tp")
    tokens, model_width = out_grad.shape
    per_token = routes.shape[1]
    capacity = routed_inputs.shape[3]
    gate_probs = jax.nn.softmax(chosen_logits, axis=-1)
    slot_index = slot_places(routes, experts, capacity)
    inputs = routed_inputs.reshape(-1, model_width)
    narrow = model_width // tp_count
    column_piece = lax.dynamic_slice_in_dim(out_grad, lax.axis_index("tp") * narrow, narrow, 1)
    outgoing = fill_slots(weighted_rows(column_piece, gate_probs), slot_index, experts * capacity)
    arrived = lax.all_to_all(
        outgoing.reshape(experts, capacity, narrow), "ep", split_axis=0, concat_axis=0, tiled=True
    )
    scaled = lax.all_gather(arrived.reshape(-1, narrow), "tp", axis=1, tiled=True)
    gate_full, up_full, down_full = gather_together((w_gate, w_up, w_down), "fsdp", (1, 1, 2))
    gate_full = gate_full[0]
    up_full = up_full[0]
    down_full = down_full[0]
    gate_act = jnp.dot(inputs, gate_full, preferred_element_type=jnp.float32)
    up_act = jnp.dot(inputs, up_full, preferred_element_type=jnp.float32)
    sigmoid_gate = jax.nn.sigmoid(gate_act)
    silu_gate = gate_act * sigmoid_gate
    hidden = (silu_gate * up_act).astype(jnp.bfloat16)
    hidden_grad = contract_last(scaled, down_full)
    products = jnp.sum(hidden_grad * hidden.astype(jnp.float32), axis=1)
    up_grad = (hidden_grad * silu_gate).astype(jnp.bfloat16)
    gate_grad = (
        hidden_grad * up_act * sigmoid_gate * (1.0 + gate_act * (1.0 - sigmoid_gate))
    ).astype(jnp.bfloat16)
    slot_part = contract_last(gate_grad, gate_full) + contract_last(up_grad, up_full)
    pair_grads = jnp.concatenate([gate_grad, up_grad], axis=1)

    def grad_term(first_row, row_count):
        input_cols = lax.dynamic_slice_in_dim(inputs, first_row, row_count, 1)
        scaled_cols = lax.dynamic_slice_in_dim(scaled, first_row, row_count, 1)
        gate_up_part = transpose_dot(input_cols, pair_grads)
        down_part = transpose_dot(scaled_cols, hidden)
        return jnp.concatenate([gate_up_part, down_part], axis=1)

    grad_rows = own_rows(grad_term, model_width // lax.axis_size("fsdp"), "fsdp")
    hidden_units = hidden.shape[1]
    grad_gate = grad_rows[:, :hidden_units][None]
    grad_up = grad_rows[:, hidden_units : 2 * hidden_units][None]
    grad_down = grad_rows[:, 2 * hidden_units :].T[None]
    narrow = model_width // tp_count
    column_sum = lax.psum_scatter(
        slot_part.astype(jnp.bfloat16), "tp", scatter_dimension=1, tiled=True
    ).astype(jnp.float32)
    product_sum = lax.psum(products.astype(jnp.bfloat16), "tp").astype(jnp.float32)
    leaving = (
        column_sum.astype(jnp.bfloat16).reshape(experts, capacity, narrow),
        product_sum.astype(jnp.bfloat16).reshape(experts, capacity),
    )
    back_rows, back_products = (
        lax.all_to_all(leaving[0], "ep", split_axis=0, concat_axis=0, tiled=True),
        lax.all_to_all(leaving[1], "ep", split_axis=0, concat_axis=0, tiled=True),
    )
    combined = combine(back_rows.reshape(-1, narrow), slot_index, tokens, per_token)
    input_grad = lax.all_gather(combined, "tp", axis=1, tiled=True)
    chosen = (
        jnp.take(back_products.reshape(-1), slot_index)
        .astype(jnp.float32)
        .reshape(tokens, per_token)
    )
    logit_grad = chosen - gate_probs * jnp.sum(chosen, axis=1, keepdims=True)
    return (input_grad, logit_grad, grad_gate, grad_up, grad_down)


def solution(mesh):
    return jax.shard_map(
        on_device,
        mesh=mesh,
        in_specs=(
            P(("ep", "fsdp"), None),
            P(("ep", "fsdp"), None),
            P(("ep", "fsdp"), None),
            P("ep", None, "fsdp", None, None),
            P("ep", "fsdp", "tp"),
            P("ep", "fsdp", "tp"),
            P("ep", "tp", "fsdp"),
        ),
        out_specs=(
            P(("ep", "fsdp"), None),
            P(("ep", "fsdp"), None),
            P("ep", "fsdp", "tp"),
            P("ep", "fsdp", "tp"),
            P("ep", "tp", "fsdp"),
        ),
        check_vma=False,
    )
```

profile of v0, /device:TPU:1, one launch (start us, length us, event | category | flops | bytes accessed | tf_op | source)
XLA Modules:
  0.0 340.7 jit_solution(7325050296816589945)
XLA Ops:
  18.4 2.1 gather_fusion
  20.6 37.3 %all_to_all.19 = bf16[16,32,1024]{2,1,0:T(8,128)(2,1)} all-to-all(bf16[16,32,1024]{2,1,0:T(8,128)(2,1)S(1)} %broadcast_select_fusion), channel_id=1, replica_groups=mesh['ep'=16,'fsdp'=4,'tp'=4] {'ep'}, dimensions={0} | all-to-all | bytes 2097152 | tf_op jit(solution)/shard_map/all_to_all | solution.py:80
  58.1 26.2 %all-gather.9.cloned.1.call-done = bf16[3145728]{0:T(1024)(128)(2,1)} async-done(((bf16[786432]{0:T(1024)(128)(2,1)}), bf16[3145728]{0:T(1024)(128)(2,1)}) %all-gather.9.cloned.1.call-update) | async-done | bytes 6291472 | tf_op jit(solution)/shard_map/all_gather | solution.py:15
  84.3 7.8 %reshape.171 = bf16[4,786432]{1,0:T(4,128)(2,1)} reshape(bf16[3145728]{0:T(1024)(128)(2,1)} %all-gather.9.cloned.1.call-done) | data formatting | bytes 12582912 | tf_op jit(solution)/shard_map/all_gather | solution.py:15
  92.1 5.4 %fusion.15 = (bf16[4,262144]{1,0:T(4,128)(2,1)}, bf16[4,262144]{1,0:T(4,128)(2,1)S(1)}, bf16[4,262144]{1,0:T(4,128)(2,1)}) fusion(bf16[4,786432]{1,0:T(4,128)(2,1)} %reshape.171), kind=kLoop, calls=%fused_computation.56 | loop fusion | bytes 12582912 | tf_op jit(solution)/shard_map/slice | solution.py:17
  97.5 3.3 squeeze_reshape_transpose_reshape.7
  100.7 3.5 %squeeze_reshape_transpose_reshape.6 = bf16[4096,256]{1,0:T(8,128)(2,1)S(1)} reshape(bf16[4,262144]{1,0:T(4,128)(2,1)} %get-tuple-element.34) | data formatting | bytes 4194304 | tf_op jit(solution)/shard_map/squeeze;reshape;transpose;reshape | solution.py:86
  104.2 3.6 %copy.64 = bf16[1,4,256,1024]{3,2,1,0:T(8,128)(2,1)} copy(bf16[1,4,256,1024]{3,1,2,0:T(4,128)(2,1)} %bitcast.71) | data formatting | bytes 4194304
  107.8 3.9 %copy.52 = bf16[1,256,4,1024]{1,3,2,0:T(8,128)(2,1)} copy(bf16[1,256,4,1024]{3,1,2,0:T(8,128)(2,1)} %bitcast.70) | data formatting | bytes 4194304 | tf_op jit(solution)/shard_map/transpose | solution.py:10
  111.7 4.3 %convolution_bitcast_fusion = f32[512,256]{0,1:T(8,128)S(1)} fusion(bf16[4096,256]{1,0:T(8,128)(2,1)} %squeeze_reshape_transpose_reshape.7, bf16[512,4096]{1,0:T(8,128)(2,1)} %bitcast.85), kind=kOutput, calls=%fused_computation.11 | convolution fusion | flops 1073741824 | bytes 6815744 | tf_op jit(solution)/shard_map/dot_general | solution.py:88
  116.0 2.1 convolution_bitcast_fusion.1
  118.1 19.4 %all-gather.5.cloned.1.call-done = bf16[512,4096]{1,0:T(8,128)(2,1)} async-done(((bf16[512,1024]{1,0:T(8,128)(2,1)}), bf16[512,4096]{1,0:T(8,128)(2,1)}) %all-gather.5.cloned.1.call-update) | async-done | bytes 4194320 | tf_op jit(solution)/shard_map/all_gather | solution.py:83
  137.5 4.5 %multiply_reduce_fusion = (bf16[512]{0:T(512)(128)(2,1)S(1)}, bf16[512,256]{0,1:T(8,128)(2,1)S(1)}, bf16[512,256]{0,1:T(8,128)(2,1)S(1)}, bf16[512,256]{0,1:T(8,128)(2,1)S(1)}) fusion(f32[512,256]{0,1:T(8,128)} %convolution_bitcast_fusion.1, f32[512,256]{0,1:T(8,128)S(1)} %convolution_bitcast_fusion, bf16[512,4096]{1,0:T(8,128)(2,1)} %all-gather.5.cloned.1.call-done, ...), kind=kOutput, calls=%fused_computation.23 | convolution fusion | flops 1076100608 | bytes 8127488 | tf_op jit(solution)/shard_map/dot_general | solution.py:63
  143.4 3.4 add_convert_fusion
  146.9 6.6 %psum.7 = bf16[16,1,32]{2,0,1:T(8,128)(2,1)S(1)} all-reduce(bf16[16,1,32]{2,0,1:T(8,128)(2,1)S(1)} %all_to_all.14), channel_id=1, replica_groups=mesh['ep'=16,'fsdp'=4,'tp'=4] {'tp'}, use_global_device_ids=true, to_apply=%region_9.10 | all-reduce | flops 512 | bytes 2048 | tf_op jit(solution)/shard_map/psum | solution.py:118
  153.5 17.0 %all_to_all.20 = bf16[16,1,32]{2,1,0:T(2,128)(2,1)S(1)} all-to-all(bf16[16,1,32]{2,1,0:T(2,128)(2,1)S(1)} %copy.53), channel_id=1, replica_groups=mesh['ep'=16,'fsdp'=4,'tp'=4] {'ep'}, dimensions={0} | all-to-all | bytes 2048 | tf_op jit(solution)/shard_map/all_to_all | solution.py:125
  170.5 26.2 %reduce-scatter.3.cloned.1.call-done = bf16[512,1024]{1,0:T(8,128)(2,1)} async-done(((bf16[512,4096]{1,0:T(8,128)(2,1)}), bf16[512,1024]{1,0:T(8,128)(2,1)}) %reduce-scatter.3.cloned.1.call-update) | async-done | bytes 1048592 | tf_op jit(solution)/shard_map/reduce_scatter | solution.py:115
  196.7 7.9 %all-to-all-start.1 = ((bf16[16,32,1024]{2,1,0:T(8,128)(2,1)}), bf16[16,32,1024]{2,1,0:T(8,128)(2,1)S(1)}, u32[]{:S(2)}, u32[]{:S(2)}) async-start(bf16[16,32,1024]{2,1,0:T(8,128)(2,1)} %bitcast.78), calls=%async_computation.2 | async-start | bytes 2097152 | tf_op jit(solution)/shard_map/all_to_all | solution.py:124
  207.4 25.3 %all-to-all-done.1 = bf16[16,32,1024]{2,1,0:T(8,128)(2,1)S(1)} async-done(((bf16[16,32,1024]{2,1,0:T(8,128)(2,1)}), bf16[16,32,1024]{2,1,0:T(8,128)(2,1)S(1)}, u32[]{:S(2)}, u32[]{:S(2)}) %all-to-all-start.1) | async-done | bytes 1048608 | tf_op jit(solution)/shard_map/all_to_all | solution.py:124
  236.3 3.7 %convolution_convert_fusion.1 = bf16[4096,256]{0,1:T(8,128)(2,1)S(1)} fusion(bf16[512,256]{0,1:T(8,128)(2,1)S(1)} %get-tuple-element.33, bf16[512,4096]{1,0:T(8,128)(2,1)} %all-gather.5.cloned.1.call-done), kind=kOutput, calls=%fused_computation.8 | convolution fusion | flops 1074790400 | bytes 6553600 | tf_op jit(solution)/shard_map/dot_general | solution.py:57
  240.0 2.4 fusion
  242.4 3.4 %pad_maximum_fusion = bf16[4096,768]{0,1:T(8,128)(2,1)} fusion(bf16[4096,256]{0,1:T(8,128)(2,1)S(1)} %convolution_convert_fusion.1, bf16[4096,512]{0,1:T(8,128)(2,1)S(1)} %fusion), kind=kLoop, calls=%fused_computation.5 | loop fusion | flops 12582912 | bytes 12582912 | tf_op jit(solution)/shard_map/concatenate | solution.py:107
  246.4 9.8 %all-gather.7.cloned.1.call-done = bf16[128,4096]{1,0:T(8,128)(2,1)} async-done(((bf16[128,1024]{1,0:T(8,128)(2,1)}), bf16[128,4096]{1,0:T(8,128)(2,1)}) %all-gather.7.cloned.1.call-update) | async-done | bytes 1048592 | tf_op jit(solution)/shard_map/all_gather | solution.py:128
  256.2 71.4 %reduce-scatter.5.cloned.1.call-done = bf16[1024,768]{0,1:T(8,128)(2,1)} async-done(((bf16[4096,768]{0,1:T(8,128)(2,1)}), bf16[1024,768]{0,1:T(8,128)(2,1)}) %reduce-scatter.5.cloned.1.call-update) | async-done | bytes 1572880 | tf_op jit(solution)/shard_map/reduce_scatter | solution.py:25
  (78 shorter events, 26.3 us)
Async XLA Ops:
  7.2 77.2 %all-gather.9.cloned.1.call-start = ((), (), s32[]{:S(2)}) async-start(), calls=%async_computation.9 | async-start | bytes 7864320 | tf_op jit(solution)/shard_map/all_gather | solution.py:15
  10.1 2.5 copy-start.3
  12.5 2.6 copy-start.2
  12.6 125.0 %all-gather.5.cloned.1.call-start = ((), (), s32[]{:S(2)}) async-start(), calls=%async_computation.5 | async-start | bytes 5242880 | tf_op jit(solution)/shard_map/all_gather | solution.py:83
  57.9 138.8 %reduce-scatter.3.cloned.1.call-start = ((), (), s32[]{:S(2)}) async-start(), calls=%async_computation.6 | async-start | bytes 5242880 | tf_op jit(solution)/shard_map/reduce_scatter | solution.py:115
  111.7 4.3 %copy-start.4 = (bf16[1,16,1,32,4096]{4,3,2,1,0:T(8,128)(2,1)S(1)}, bf16[1,16,1,32,4096]{4,3,2,1,0:T(8,128)(2,1)}, u32[]{:S(2)}) copy-start(bf16[1,16,1,32,4096]{4,3,2,1,0:T(8,128)(2,1)} %param.10) | copy-start | bytes 12582916
  137.5 4.5 %copy-start = (bf16[4096,256]{1,0:T(8,128)(2,1)S(1)}, bf16[4096,256]{1,0:T(8,128)(2,1)}, u32[]{:S(2)}) copy-start(bf16[4096,256]{1,0:T(8,128)(2,1)} %squeeze_reshape_transpose_reshape.7) | copy-start | bytes 6291460
  196.7 36.0 %all-to-all-start.1 = ((bf16[16,32,1024]{2,1,0:T(8,128)(2,1)}), bf16[16,32,1024]{2,1,0:T(8,128)(2,1)S(1)}, u32[]{:S(2)}, u32[]{:S(2)}) async-start(bf16[16,32,1024]{2,1,0:T(8,128)(2,1)} %bitcast.78), calls=%async_computation.2 | async-start | bytes 2097152 | tf_op jit(solution)/shard_map/all_to_all | solution.py:124
  204.6 51.6 %all-gather.7.cloned.1.call-start = ((), (), s32[]{:S(2)}) async-start(), calls=%async_computation.7 | async-start | bytes 1310720 | tf_op jit(solution)/shard_map/all_gather | solution.py:128
  236.0 91.7 %reduce-scatter.5.cloned.1.call-start = ((), (), s32[]{:S(2)}) async-start(), calls=%async_computation.8 | async-start | bytes 7864320 | tf_op jit(solution)/shard_map/reduce_scatter | solution.py:25
  236.3 3.7 %copy-start.5 = (bf16[1,16,1,32,4096]{4,3,2,1,0:T(8,128)(2,1)S(1)}, bf16[1,16,1,32,4096]{4,3,2,1,0:T(8,128)(2,1)}, u32[]{:S(2)}) copy-start(bf16[1,16,1,32,4096]{4,3,2,1,0:T(8,128)(2,1)} %param.10) | copy-start | bytes 12582916
  330.6 2.6 copy-start.1
Sparse Core Ops, SparseCore 0:
  12.7 71.5 all-gather.8
  86.1 51.3 all-gather.4
  146.9 49.7 reduce-scatter.2
  236.1 20.0 all-gather.6
  258.6 68.9 reduce-scatter.4
where the time goes:
time: 341 us
  waiting for transfers between devices  178 us (52%)
  blocking collectives  60.9 us (18%)
  local copies, waits for them, and re-layouts  46.1 us (14%)
  matrix products  21.6 us (6%)
  between operations  14.1 us (4%)
  other arithmetic  11.1 us (3%)
  starting transfers between devices  8.59 us (3%)
    reduce_scatter x1, waiting for transfers between devices, own_rows(): lax.psum_scatter(whole, axis, scatter_dimension=0, tiled=True)  71.4 us
    all_to_all x1, blocking collectives, on_device(): lax.all_to_all(outgoing.reshape(experts, capacity, narrow), 'ep', split_a...  37.3 us
    all_gather x1, waiting for transfers between devices, gather_together(): lines, at, outs = (lax.all_gather(ravelled, axis), 0, [])  26.2 us
    reduce_scatter x1, waiting for transfers between devices, on_device(): lax.psum_scatter(slot_part.astype(jnp.bfloat16), 'tp', scatter_dimension=...  26.2 us
    all_to_all x1, waiting for transfers between devices, on_device(): lax.all_to_all(leaving[0], 'ep', split_axis=0, concat_axis=0, tiled=True)  25.3 us
    all_gather x1, waiting for transfers between devices, on_device(): lax.all_gather(arrived.reshape(-1, narrow), 'tp', axis=1, tiled=True)  19.4 us
    all_to_all x1, blocking collectives, on_device(): lax.all_to_all(leaving[1], 'ep', split_axis=0, concat_axis=0, tiled=True)  17 us
    unnamed x20, local copies, waits for them, and re-layouts  11.3 us
  transfers between devices with their start and end apart: 6, of which 6 were waited for; matrix products, arithmetic and copies ran while one was open for 16% of the time, Pallas kernels for 0%

commit v1 on v0

v1 whole, which is shorter than its diff:
```python
import functools

import jax
import jax.numpy as jnp
from jax import lax
from jax.experimental import pallas as pl
from jax.experimental.pallas import tpu as pltpu
from jax.sharding import PartitionSpec as P

MESH = pl.DeviceIdType.MESH
F32, BF16, I32 = jnp.float32, jnp.bfloat16, jnp.int32

DZ = (0, 1, -1, 2, -2, 3, -3, 4)
NJ = 16
CAP = 32
TOK = 128
NCH = 4
ROWS = 128
SLOTS = 512
Q = 1024
FFL = 256


def dot_nn(a, b):
    return lax.dot_general(a, b, (((1,), (0,)), ((), ())), preferred_element_type=F32)


def dot_nt(a, b):
    return lax.dot_general(a, b, (((1,), (1,)), ((), ())), preferred_element_type=F32)


def kernel(
    routes, logits, og, x, wg, wu, wd,
    ig_o, lg_o, gg_o, gu_o, gd_o,
    xb, xt, wgb, wub, wdb, ogq, outb, sb,
    act_a, act_b, hg, hid, hidt, ggb, gub,
    qs, qt, q01, psb, m16, p16, c16,
    y1s, y1r, y2s, y2r, sown, ret, back,
    x1g, x1u, x1d, x1gr, x1ur, x1dr, x2g, x2u, x2d, x2gr, x2ur, x2dr, owng, ownu, ownd,
    fin, prt, prr, cs, cr,
    lx, lw, lo, so,
    xa_s, xa_r, xf_s, xf_r, x1_s, x1_rs, x2_s, x2_rs,
    ya_s, ya_r, yf_s, yf_r, y1_s, y1_rs, y2_s, y2_rs,
    za_s, za_r, zb_s, zb_r, zp_s, zp_r, fa_s, fa_r, ff_s, ff_r, c_s, c_r,
):
    ep = lax.axis_index("ep")
    f = lax.axis_index("fsdp")
    t = lax.axis_index("tp")
    z = ep // 2
    core = ep % 2

    def up(v):
        return (v + 1) % 4

    def down(v):
        return (v + 3) % 4

    xn = (up(f), down(f))
    yn = (up(t), down(t))

    def source_of(j):
        return ((z + DZ[j // 2] + 8) % 8) * 2 + (core + j % 2) % 2

    def expert_of(j):
        return ((z - DZ[j // 2] + 8) % 8) * 2 + (core + j % 2) % 2

    def remote(src, dst, ss, rs, **axis):
        return pltpu.make_async_remote_copy(
            src_ref=src, dst_ref=dst, send_sem=ss, recv_sem=rs, device_id=axis, device_id_type=MESH
        )

    tq = pl.multiple_of(t * Q, Q)
    l_og = pltpu.make_async_copy(og.at[:, pl.ds(tq, Q)], ogq, lo.at[0])
    l_w = [
        pltpu.make_async_copy(src, dst.at[f], lw.at[m])
        for m, (src, dst) in enumerate(((wg, wgb), (wu, wub), (wd, wdb)))
    ]
    l_w[0].start()
    l_w[1].start()
    l_og.start()
    l_x = [
        pltpu.make_async_copy(x.at[source_of(j)], xb.at[pl.ds(CAP * j, CAP), :], lx.at[j])
        for j in range(NJ)
    ]

    barrier = pltpu.get_barrier_semaphore()
    for k in (1, 3):
        pl.semaphore_signal(barrier, inc=1, device_id={"fsdp": (f + k) % 4}, device_id_type=MESH)
    for k in (1, 2, 3):
        pl.semaphore_signal(barrier, inc=1, device_id={"tp": (t + k) % 4}, device_id_type=MESH)
    for j in range(1, NJ):
        pl.semaphore_signal(barrier, inc=1, device_id={"ep": (ep + j) % 16}, device_id_type=MESH)
    l_w[2].start()
    for c in l_x:
        c.start()
    pl.semaphore_wait(barrier, 20)

    WB = (wgb, wub, wdb)
    HALF = (512, 512, 128)
    xa = [[remote(WB[m].at[f], WB[m].at[f], xa_s.at[m, d], xa_r.at[m, d], fsdp=xn[d]) for d in range(2)] for m in range(3)]

    def half_of(m, d, b):
        return WB[m].at[b, pl.ds(d * HALF[m], HALF[m]), :]

    fsrc = (down(f), up(f))
    xf = [
        [remote(half_of(m, d, fsrc[d]), half_of(m, d, fsrc[d]), xf_s.at[m, d], xf_r.at[m, d], fsdp=xn[d]) for d in range(2)]
        for m in range(3)
    ]

    def start(pair):
        for c in pair:
            c.start()

    for m in (0, 1):
        l_w[m].wait()
        start(xa[m])

    r0, r1 = routes[0:1, :], routes[1:2, :]
    g0, g1 = logits[0:1, :], logits[1:2, :]
    gm = jnp.maximum(g0, g1)
    e0, e1 = jnp.exp(g0 - gm), jnp.exp(g1 - gm)
    p0, p1 = e0 / (e0 + e1), e1 / (e0 + e1)
    jj = lax.broadcasted_iota(I32, (NJ, TOK), 0)
    ii = jj // 2
    dz = jnp.where(ii % 2 == 1, (ii + 1) // 2, -(ii // 2))
    ee = ((z - dz + 8) % 8) * 2 + (core + jj % 2) % 2
    h0, h1 = r0 == ee, r1 == ee
    m16[...] = jnp.where(h0, 1.0, 0.0) + jnp.where(h1, 2.0, 0.0)
    p16[...] = jnp.where(h0, p0, 0.0) + jnp.where(h1, p1, 0.0)
    taken = jnp.where(h0 | h1, 1.0, 0.0).astype(BF16)
    tri = jnp.where(
        lax.broadcasted_iota(I32, (TOK, TOK), 0) < lax.broadcasted_iota(I32, (TOK, TOK), 1), 1.0, 0.0
    ).astype(BF16)
    c16[...] = dot_nn(taken, tri)
    place = lax.broadcasted_iota(I32, (CAP, TOK), 0).astype(F32)
    for j in range(NJ):
        rows = pl.ds(CAP * j, CAP)
        code = m16[j : j + 1, :]
        here = c16[j : j + 1, :] == place
        one0 = jnp.where(here & (code == 1.0), 1.0, 0.0)
        one1 = jnp.where(here & (code == 2.0), 1.0, 0.0)
        q01[0, rows, :] = one0
        q01[1, rows, :] = one1
        one = one0 + one1
        qs[rows, :] = one.astype(BF16)
        psb[rows, :] = jnp.broadcast_to(jnp.sum(one * p16[j : j + 1, :], axis=1, keepdims=True), (CAP, TOK))
    l_og.wait()
    for c in range(NCH):
        rows = pl.ds(ROWS * c, ROWS)
        picked = dot_nn(qs[rows, :], ogq[...])
        outb[rows, :] = (picked * psb[rows, 0:1]).astype(BF16)

    za = [None] + [
        remote(
            outb.at[pl.ds(CAP * j, CAP), :], sb.at[t, pl.ds(CAP * j, CAP), :],
            za_s.at[j], za_r.at[j], ep=expert_of(j),
        )
        for j in range(1, NJ)
    ]
    for j in range(1, NJ):
        za[j].start()
    sb[t, 0:CAP, :] = outb[0:CAP, :]

    def add_block(dst, w, b, first):
        cols = pl.ds(pl.multiple_of(b * Q, Q), Q)

        @pl.loop(0, 2)
        def _(i):
            rows = pl.ds(pl.multiple_of(i * 256, 256), 256)
            part = dot_nn(xb[rows, cols], w[b])
            if first:
                dst[rows, :] = part
            else:
                dst[rows, :] += part

    for c in l_x:
        c.wait()
    add_block(act_a, wgb, f, True)

    ya = [
        [
            remote(sb.at[t, pl.ds(ROWS * c, ROWS), :], sb.at[t, pl.ds(ROWS * c, ROWS), :], ya_s.at[c, d], ya_r.at[c, d], tp=yn[d])
            for d in range(2)
        ]
        for c in range(NCH)
    ]
    tsrc = (down(t), up(t))

    def s_half(c, d):
        return sb.at[tsrc[d], pl.ds(ROWS * c + 64 * d, 64), :]

    yf = [[remote(s_half(c, d), s_half(c, d), yf_s.at[c, d], yf_r.at[c, d], tp=yn[d]) for d in range(2)] for c in range(NCH)]

    def rows_arrived(c):
        for j in range(max(1, 4 * c), 4 * c + 4):
            za[j].wait_recv()
        start(ya[c])

    def recv(pair):
        for c in pair:
            c.wait_recv()

    rows_arrived(0)
    add_block(act_b, wub, f, True)
    rows_arrived(1)
    recv(xa[0])
    start(xf[0])
    l_w[2].wait()
    start(xa[2])
    recv(ya[0])
    start(yf[0])
    add_block(act_a, wgb, up(f), False)
    add_block(act_a, wgb, down(f), False)
    rows_arrived(2)
    recv(ya[1])
    start(yf[1])

    def transpose_x(lo_, hi_):
        @pl.loop(lo_, hi_)
        def _(i):
            at = pl.ds(pl.multiple_of(i * 256, 256), 256)
            xt[at, :] = xb[:, at].T

    recv(xa[1])
    start(xf[1])
    add_block(act_b, wub, up(f), False)
    add_block(act_b, wub, down(f), False)
    rows_arrived(3)
    recv(ya[2])
    start(yf[2])
    transpose_x(0, 8)
    recv(xf[0])
    add_block(act_a, wgb, (f + 2) % 4, False)
    transpose_x(8, 16)
    recv(ya[3])
    start(yf[3])

    def add_hidden(b, first):
        @pl.loop(0, 2)
        def _(i):
            rows = pl.ds(pl.multiple_of(i * 256, 256), 256)
            part = dot_nt(sb[b, rows, :], wdb[b])
            if first:
                hg[rows, :] = part
            else:
                hg[rows, :] += part

    recv(xa[2])
    start(xf[2])
    for c in range(NCH):
        recv(yf[c])
    for k in (0, 1, 3):
        add_hidden((f + k) % 4, k == 0)
    qt[...] = qs[...].T
    recv(xf[1])
    add_block(act_b, wub, (f + 2) % 4, False)

    @pl.loop(0, 8)
    def _(i):
        rows = pl.ds(pl.multiple_of(i * 64, 64), 64)
        gate, upv = act_a[rows, :], act_b[rows, :]
        sig = jax.nn.sigmoid(gate)
        silu = gate * sig
        hid[rows, :] = (silu * upv).astype(BF16)
        act_a[rows, :] = silu
        act_b[rows, :] = upv * sig * (1.0 + gate * (1.0 - sig))

    hidt[...] = hid[...].T

    def x1_pair(m, s, r):
        h = HALF[m]
        return [
            remote(s.at[pl.ds(h * d, h), :], r.at[pl.ds(h * d, h), :], x1_s.at[m, d], x1_rs.at[m, d], fsdp=xn[d])
            for d in range(2)
        ]

    def x2_pair(m, s, r):
        return [remote(s.at[d], r.at[d], x2_s.at[m, d], x2_rs.at[m, d], fsdp=xn[d]) for d in range(2)]

    x1 = [x1_pair(0, x1g, x1gr), x1_pair(1, x1u, x1ur), x1_pair(2, x1d, x1dr)]
    x2 = [x2_pair(0, x2g, x2gr), x2_pair(1, x2u, x2ur), x2_pair(2, x2d, x2dr)]

    def down_grad(b, put):
        @pl.loop(0, 2)
        def _(i):
            cols = pl.ds(pl.multiple_of(i * 512, 512), 512)
            put(slice(None), cols, dot_nn(hidt[...], sb[b, :, cols]))

    def wide_grad(b, g, put):
        @pl.loop(0, 4)
        def _(i):
            rows = pl.ds(pl.multiple_of(i * 256, 256), 256)
            at = pl.ds(pl.multiple_of(b * Q + i * 256, 256), 256)
            put(rows, slice(None), dot_nn(xt[at, :], g[...]))

    def store_bf16(dst):
        def put(rows, cols, v):
            dst[rows, cols] = v.astype(BF16)

        return put

    def store_f32(dst):
        def put(rows, cols, v):
            dst[rows, cols] = v

        return put

    def add_half(m, dst, got):
        h = HALF[m]
        step = h // 2
        for d in range(2):

            @pl.loop(0, 2)
            def _(i):
                rows = pl.ds(pl.multiple_of(h * d + i * step, 64), step)
                dst[d, rows, :] = (dst[d, rows, :].astype(F32) + got[rows, :].astype(F32)).astype(BF16)

    down_grad((f + 2) % 4, store_bf16(x1d))
    start(x1[2])
    down_grad(up(f), store_bf16(x2d.at[0]))
    down_grad(down(f), store_bf16(x2d.at[1]))

    recv(xf[2])
    add_hidden((f + 2) % 4, False)

    for c in range(NCH):
        rows = pl.ds(ROWS * c, ROWS)
        h = hg[rows, :]
        gub[rows, :] = (h * act_a[rows, :]).astype(BF16)
        ggb[rows, :] = (h * act_b[rows, :]).astype(BF16)
        prod = jnp.sum(h * hid[rows, :].astype(F32), axis=1, keepdims=True)
        prt[c] = jnp.broadcast_to(prod, (ROWS, 128)).T[0:8, :]

    y1 = [
        [
            remote(y1s.at[c, pl.ds(64 * d, 64), :], y1r.at[c, pl.ds(64 * d, 64), :], y1_s.at[c, d], y1_rs.at[c, d], tp=yn[d])
            for d in range(2)
        ]
        for c in range(NCH)
    ]
    y2 = [[remote(y2s.at[c, d], y2r.at[c, d], y2_s.at[c, d], y2_rs.at[c, d], tp=yn[d]) for d in range(2)] for c in range(NCH)]

    def slot_block(c, b):
        rows = pl.ds(ROWS * c, ROWS)
        return dot_nt(ggb[rows, :], wgb[b]) + dot_nt(gub[rows, :], wub[b])

    def slot_first(c):
        y1s[c] = slot_block(c, (t + 2) % 4).astype(BF16)
        start(y1[c])

    def slot_rest(c):
        y2s[c, 0] = slot_block(c, up(t)).astype(BF16)
        y2s[c, 1] = slot_block(c, down(t)).astype(BF16)
        sown[pl.ds(ROWS * c, ROWS), :] = slot_block(c, t)

    def slot_second(c):
        recv(y1[c])
        for d in range(2):
            rows = pl.ds(64 * d, 64)
            y2s[c, d, rows, :] = (y2s[c, d, rows, :].astype(F32) + y1r[c, rows, :].astype(F32)).astype(BF16)
        start(y2[c])

    zb = [None] + [
        remote(ret.at[pl.ds(CAP * j, CAP), :], back.at[pl.ds(CAP * j, CAP), :], zb_s.at[j], zb_r.at[j], ep=source_of(j))
        for j in range(1, NJ)
    ]
    zp = [None] + [remote(prt.at[j // 4], prr.at[j], zp_s.at[j], zp_r.at[j], ep=source_of(j)) for j in range(1, NJ)]

    def slot_done(c):
        recv(y2[c])
        rows = pl.ds(ROWS * c, ROWS)
        total = sown[rows, :] + y2r[c, 0].astype(F32) + y2r[c, 1].astype(F32)
        ret[rows, :] = total.astype(BF16)
        for j in range(max(1, 4 * c), 4 * c + 4):
            zb[j].start()
        if c == 0:
            back[0:CAP, :] = ret[0:CAP, :]

    slot_first(3)
    wide_grad((f + 2) % 4, ggb, store_bf16(x1g))
    start(x1[0])
    slot_first(2)
    recv(x1[2])
    add_half(2, x2d, x1dr)
    start(x2[2])
    wide_grad((f + 2) % 4, gub, store_bf16(x1u))
    start(x1[1])
    slot_rest(3)
    slot_second(3)
    slot_first(1)
    slot_rest(2)
    slot_second(2)
    slot_first(0)
    for j in range(1, NJ):
        zp[j].start()
    prr[0] = prt[0]
    wide_grad(up(f), ggb, store_bf16(x2g.at[0]))
    wide_grad(down(f), ggb, store_bf16(x2g.at[1]))
    slot_rest(1)
    slot_second(1)
    recv(x1[0])
    add_half(0, x2g, x1gr)
    start(x2[0])
    slot_done(3)
    slot_rest(0)
    slot_second(0)
    wide_grad(up(f), gub, store_bf16(x2u.at[0]))
    wide_grad(down(f), gub, store_bf16(x2u.at[1]))
    recv(x1[1])
    add_half(1, x2u, x1ur)
    start(x2[1])
    slot_done(2)
    down_grad(f, store_f32(ownd))
    wide_grad(f, ggb, store_f32(owng))
    wide_grad(f, gub, store_f32(ownu))
    slot_done(1)

    outs = [
        pltpu.make_async_copy(owng, gg_o, so.at[0]),
        pltpu.make_async_copy(ownu, gu_o, so.at[1]),
        pltpu.make_async_copy(ownd, gd_o, so.at[2]),
    ]

    def finish(m, own, got):
        recv(x2[m])
        n = own.shape[0] // 4

        @pl.loop(0, 4)
        def _(i):
            rows = pl.ds(pl.multiple_of(i * n, 64), n)
            own[rows, :] = own[rows, :] + got[0, rows, :].astype(F32) + got[1, rows, :].astype(F32)

        outs[m].start()

    finish(2, ownd, x2dr)

    for j in range(1, NJ):
        zp[j].wait_recv()
    lane = lax.broadcasted_iota(I32, (8, 128), 1) // CAP
    ch = [jnp.zeros((8, TOK), F32), jnp.zeros((8, TOK), F32)]
    for c in range(NCH):
        row = jnp.zeros((8, 128), F32)
        for i in range(4):
            row = jnp.where(lane == i, prr[4 * c + i], row)
        for k in range(2):
            ch[k] = ch[k] + lax.dot_general(
                row, q01[k, pl.ds(ROWS * c, ROWS), :], (((1,), (0,)), ((), ())),
                precision=lax.Precision.HIGHEST, preferred_element_type=F32,
            )
    half8 = lax.broadcasted_iota(I32, (8, TOK), 0)
    cs[...] = jnp.where(half8 == 0, ch[0], ch[1])
    cc = [
        remote(cs, cr.at[t], c_s.at[k - 1], c_r.at[k - 1], tp=(t + k) % 4) for k in (1, 2, 3)
    ]
    start(cc)
    cr[t] = cs[...]

    slot_done(0)

    for j in range(1, NJ):
        zb[j].wait_recv()

    for i in range(2):
        cols = pl.ds(512 * i, 512)
        fin[t, :, cols] = dot_nn(qt[...], back[:, cols]).astype(BF16)
    fa = [remote(fin.at[t], fin.at[t], fa_s.at[d], fa_r.at[d], tp=yn[d]) for d in range(2)]

    def f_half(d):
        return fin.at[tsrc[d], pl.ds(64 * d, 64), :]

    ffw = [remote(f_half(d), f_half(d), ff_s.at[d], ff_r.at[d], tp=yn[d]) for d in range(2)]
    start(fa)
    recv(cc)
    total = ((cr[0] + cr[1]) + cr[2]) + cr[3]
    chosen = total.astype(BF16).astype(F32)
    both = chosen[0:1, :] + chosen[1:2, :]
    pp = jnp.where(half8 == 0, p0, p1)
    lg_o[...] = chosen - pp * both
    finish(0, owng, x2gr)
    o_own = pltpu.make_async_copy(fin.at[t], ig_o.at[:, pl.ds(tq, Q)], so.at[3])
    o_own.start()
    recv(fa)
    start(ffw)
    o_nb = []
    for d in range(2):
        at = pl.multiple_of(tsrc[d] * Q, Q)
        o_nb.append(pltpu.make_async_copy(fin.at[tsrc[d]], ig_o.at[:, pl.ds(at, Q)], so.at[4 + d]))
    start(o_nb)
    finish(1, ownu, x2ur)
    recv(ffw)
    opp = (t + 2) % 4
    o_op = pltpu.make_async_copy(fin.at[opp], ig_o.at[:, pl.ds(pl.multiple_of(opp * Q, Q), Q)], so.at[6])
    o_op.start()

    for group in (xa, xf, x1, x2, ya, yf, y1, y2):
        for pair in group:
            for c in pair:
                c.wait_send()
    for group in (za[1:], zb[1:], zp[1:], fa, ffw, cc):
        for c in group:
            c.wait_send()
    for c in outs + [o_own, o_op] + o_nb:
        c.wait()


def on_device(out_grad, routes, chosen_logits, routed_inputs, w_gate, w_up, w_down):
    hbm = pl.BlockSpec(memory_space=pl.ANY)
    vmem = pl.BlockSpec(memory_space=pltpu.VMEM)
    dma = pltpu.SemaphoreType.DMA

    def v(*shape, dtype=BF16):
        return pltpu.VMEM(shape, dtype)

    scratch = [
        v(SLOTS, 4 * Q), v(4 * Q, SLOTS), v(4, Q, FFL), v(4, Q, FFL), v(4, FFL, Q),
        v(TOK, Q), v(SLOTS, Q), v(4, SLOTS, Q),
        v(SLOTS, FFL, dtype=F32), v(SLOTS, FFL, dtype=F32), v(SLOTS, FFL, dtype=F32),
        v(SLOTS, FFL), v(FFL, SLOTS), v(SLOTS, FFL), v(SLOTS, FFL),
        v(SLOTS, TOK), v(TOK, SLOTS), v(2, SLOTS, TOK, dtype=F32), v(SLOTS, TOK, dtype=F32),
        v(NJ, TOK, dtype=F32), v(NJ, TOK, dtype=F32), v(NJ, TOK, dtype=F32),
        v(NCH, ROWS, Q), v(NCH, ROWS, Q), v(NCH, 2, ROWS, Q), v(NCH, 2, ROWS, Q),
        v(SLOTS, Q, dtype=F32), v(SLOTS, Q), v(SLOTS, Q),
        v(Q, FFL), v(Q, FFL), v(FFL, Q), v(Q, FFL), v(Q, FFL), v(FFL, Q),
        v(2, Q, FFL), v(2, Q, FFL), v(2, FFL, Q), v(2, Q, FFL), v(2, Q, FFL), v(2, FFL, Q),
        v(Q, FFL, dtype=F32), v(Q, FFL, dtype=F32), v(FFL, Q, dtype=F32),
        v(4, TOK, Q), v(NCH, 8, 128, dtype=F32), v(NJ, 8, 128, dtype=F32),
        v(8, 128, dtype=F32), v(4, 8, 128, dtype=F32),
        dma((NJ,)), dma((3,)), dma((1,)), dma((7,)),
        dma((3, 2)), dma((3, 2)), dma((3, 2)), dma((3, 2)), dma((3, 2)), dma((3, 2)), dma((3, 2)), dma((3, 2)),
        dma((4, 2)), dma((4, 2)), dma((4, 2)), dma((4, 2)), dma((4, 2)), dma((4, 2)), dma((4, 2)), dma((4, 2)),
        dma((NJ,)), dma((NJ,)), dma((NJ,)), dma((NJ,)), dma((NJ,)), dma((NJ,)),
        dma((2,)), dma((2,)), dma((2,)), dma((2,)), dma((3,)), dma((3,)),
    ]
    ig, lg, gg, gu, gd = pl.pallas_call(
        kernel,
        out_shape=(
            jax.ShapeDtypeStruct((TOK, 4 * Q), BF16),
            jax.ShapeDtypeStruct((8, 128), F32),
            jax.ShapeDtypeStruct((Q, FFL), F32),
            jax.ShapeDtypeStruct((Q, FFL), F32),
            jax.ShapeDtypeStruct((FFL, Q), F32),
        ),
        in_specs=[vmem, vmem, hbm, hbm, hbm, hbm, hbm],
        out_specs=(hbm, vmem, hbm, hbm, hbm),
        scratch_shapes=scratch,
        compiler_params=pltpu.CompilerParams(
            collective_id=0, has_side_effects=True, vmem_limit_bytes=60 * 1024 * 1024
        ),
    )(
        routes.T, chosen_logits.T, out_grad,
        routed_inputs.reshape(NJ, CAP, 4 * Q), w_gate[0], w_up[0], w_down[0],
    )
    return ig, lg[:2].T, gg[None], gu[None], gd[None]


def solution(mesh):
    return jax.shard_map(
        on_device,
        mesh=mesh,
        in_specs=(
            P(("ep", "fsdp"), None),
            P(("ep", "fsdp"), None),
            P(("ep", "fsdp"), None),
            P("ep", None, "fsdp", None, None),
            P("ep", "fsdp", "tp"),
            P("ep", "fsdp", "tp"),
            P("ep", "tp", "fsdp"),
        ),
        out_specs=(
            P(("ep", "fsdp"), None),
            P(("ep", "fsdp"), None),
            P("ep", "fsdp", "tp"),
            P("ep", "fsdp", "tp"),
            P("ep", "tp", "fsdp"),
        ),
        check_vma=False,
    )
```

time: 341 us -> 136 us (0.40)
  waiting for transfers between devices: 178 us -> 0 us
  Pallas kernels: 0 us -> 127 us
  blocking collectives: 60.9 us -> 0 us
  local copies, waits for them, and re-layouts: 46.1 us -> 7.89 us
  matrix products: 21.6 us -> 0 us
  between operations: 14.1 us -> 0.66 us
  other arithmetic: 11.1 us -> 0 us
  starting transfers between devices: 8.59 us -> 0 us
    pallas_call x0 -> x1, Pallas kernels: none -> 127 us  [on_device(): pl.pallas_call(kernel, out_shape=(jax.ShapeDtypeStruct((TOK, 4 * Q), BF16...]
    reduce_scatter x2 -> x0, waiting for transfers between devices: 97.6 us -> none  [the longest x1 71.4 us: own_rows(): lax.psum_scatter(whole, axis, scatter_dimension=0, tiled=True)]
    all_gather x3 -> x0, waiting for transfers between devices: 55.4 us -> none  [the longest x1 26.2 us: gather_together(): lines, at, outs = (lax.all_gather(ravelled, axis), 0, [])]
    all_to_all x2 -> x0, blocking collectives: 54.2 us -> none  [the longest x1 37.3 us: on_device(): lax.all_to_all(outgoing.reshape(experts, capacity, narrow), 'ep', split_a...]
    all_to_all x1 -> x0, waiting for transfers between devices: 25.3 us -> none  [on_device(): lax.all_to_all(leaving[0], 'ep', split_axis=0, concat_axis=0, tiled=True)]
    dot_general x7 -> x0, matrix products: 21.6 us -> none  [the longest x3 9.2 us: contract_last(): lax.dot_general(left, right, (((1,), (1,)), ((), ())), preferred_element_...]
    all_to_all x1 -> x0, starting transfers between devices: 7.94 us -> none  [on_device(): lax.all_to_all(leaving[0], 'ep', split_axis=0, concat_axis=0, tiled=True)]
    all_gather x1 -> x0, local copies, waits for them, and re-layouts: 7.76 us -> none  [gather_together(): lines, at, outs = (lax.all_gather(ravelled, axis), 0, [])]
  transfers between devices with their start and end apart: 6 -> 0, of which waited for: 6 -> 0; matrix products, arithmetic and copies ran while one was open for 16% -> 0% of each run, Pallas kernels for 0% -> 0%
where the time goes in v1:
time: 136 us; the launch traced here: 135 us
  Pallas kernels  127 us (93%)
  local copies, waits for them, and re-layouts  7.89 us (6%)
    pallas_call x1, Pallas kernels, on_device(): pl.pallas_call(kernel, out_shape=(jax.ShapeDtypeStruct((TOK, 4 * Q), BF16...  127 us
    unnamed x8, local copies, waits for them, and re-layouts  6.5 us

profile of v1, /device:TPU:1, one launch (start us, length us, event | category | flops | bytes accessed | tf_op | source)
XLA Modules:
  0.0 135.4 jit_solution(16351649677870231911)
XLA Ops:
  0.6 126.9 %shard_map.110 = (bf16[128,4096]{1,0:T(8,128)(2,1)}, f32[8,128]{1,0:T(8,128)}, f32[1024,256]{1,0:T(8,128)}, f32[1024,256]{1,0:T(8,128)}, f32[256,1024]{1,0:T(8,128)}) custom-call(s32[2,128]{1,0:T(2,128)} %bitcast.18, f32[2,128]{1,0:T(2,128)} %bitcast.19, bf16[128,4096]{1,0:T(8,128)(2,1)} %og.1, bf16[16,32,4096]{2,1,0:T(8,128)(2,1)} %bitcast.11, ...), custom_call_target="tpu_custom_call" | custom-call | tf_op jit(solution)/shard_map/pallas_call | solution.py:535
  127.5 0.0 copy-start.1
  127.5 0.0 copy-start
  127.5 1.4 %slice_bitcast_fusion = f32[128,2]{0,1:T(2,128)} fusion(f32[8,128]{1,0:T(8,128)} %get-tuple-element.11), kind=kLoop, calls=%fused_computation | loop fusion | bytes 2048 | tf_op jit(solution)/shard_map/transpose | solution.py:554
  128.9 2.3 %copy.16 = bf16[128,4096]{1,0:T(8,128)(2,1)} copy(bf16[128,4096]{1,0:T(8,128)(2,1)} %get-tuple-element.20) | data formatting | bytes 2097152
  131.2 2.3 %copy.17 = f32[1,1024,256]{2,1,0:T(8,128)} copy(f32[1,1024,256]{2,1,0:T(8,128)} %bitcast.14) | data formatting | bytes 2097152
  133.5 0.0 copy-done.1
  133.5 1.0 copy.18
  134.4 0.0 copy-done
  134.4 1.0 copy.19
Async XLA Ops:
  127.5 6.0 %copy-start.1 = (f32[1024,256]{1,0:T(8,128)S(1)}, f32[1024,256]{1,0:T(8,128)}, u32[]{:S(2)}) copy-start(f32[1024,256]{1,0:T(8,128)} %get-tuple-element.13) | copy-start | bytes 3145732
  127.5 6.9 %copy-start = (f32[256,1024]{1,0:T(8,128)S(1)}, f32[256,1024]{1,0:T(8,128)}, u32[]{:S(2)}) copy-start(f32[256,1024]{1,0:T(8,128)} %get-tuple-element.14) | copy-start | bytes 3145732

commit v2 on v1

--- a/solution.py
+++ b/solution.py
@@ -30,15 +30,15 @@
 
 
 def kernel(
-    routes, logits, og, x, wg, wu, wd,
+    routes_in, logits_in, og, x, wg, wu, wd,
     ig_o, lg_o, gg_o, gu_o, gd_o,
-    xb, xt, wgb, wub, wdb, ogq, outb, sb,
+    routes, logits, xb, xt, wgb, wub, wdb, ogq, outb, sb,
     act_a, act_b, hg, hid, hidt, ggb, gub,
     qs, qt, q01, psb, m16, p16, c16,
     y1s, y1r, y2s, y2r, sown, ret, back,
-    x1g, x1u, x1d, x1gr, x1ur, x1dr, x2g, x2u, x2d, x2gr, x2ur, x2dr, owng, ownu, ownd,
-    fin, prt, prr, cs, cr,
-    lx, lw, lo, so,
+    x1g, x1u, x1d, x1gr, x1ur, x1dr, x2g, x2u, x2d, x2gr, x2ur, x2dr,
+    prt, prr, cs, cr,
+    lx, lw, lo, lv,
     xa_s, xa_r, xf_s, xf_r, x1_s, x1_rs, x2_s, x2_rs,
     ya_s, ya_r, yf_s, yf_r, y1_s, y1_rs, y2_s, y2_rs,
     za_s, za_r, zb_s, zb_r, zp_s, zp_r, fa_s, fa_r, ff_s, ff_r, c_s, c_r,
@@ -71,33 +71,51 @@
 
     tq = pl.multiple_of(t * Q, Q)
     l_og = pltpu.make_async_copy(og.at[:, pl.ds(tq, Q)], ogq, lo.at[0])
+    l_r = [
+        pltpu.make_async_copy(routes_in, routes, lo.at[1]),
+        pltpu.make_async_copy(logits_in, logits, lo.at[2]),
+    ]
+    for c in l_r:
+        c.start()
+    l_og.start()
     l_w = [
         pltpu.make_async_copy(src, dst.at[f], lw.at[m])
         for m, (src, dst) in enumerate(((wg, wgb), (wu, wub), (wd, wdb)))
     ]
-    l_w[0].start()
-    l_w[1].start()
-    l_og.start()
     l_x = [
         pltpu.make_async_copy(x.at[source_of(j)], xb.at[pl.ds(CAP * j, CAP), :], lx.at[j])
         for j in range(NJ)
     ]
 
     barrier = pltpu.get_barrier_semaphore()
-    for k in (1, 3):
-        pl.semaphore_signal(barrier, inc=1, device_id={"fsdp": (f + k) % 4}, device_id_type=MESH)
-    for k in (1, 2, 3):
-        pl.semaphore_signal(barrier, inc=1, device_id={"tp": (t + k) % 4}, device_id_type=MESH)
-    for j in range(1, NJ):
-        pl.semaphore_signal(barrier, inc=1, device_id={"ep": (ep + j) % 16}, device_id_type=MESH)
-    l_w[2].start()
-    for c in l_x:
+    def tell(sem, **axis):
+        pl.semaphore_signal(sem, inc=1, device_id=axis, device_id_type=MESH)
+
+    zn = ((z + 1) % 8, (z + 7) % 8)
+    for d in range(2):
+        tell(barrier, fsdp=xn[d])
+        tell(barrier, tp=yn[d])
+        tell(barrier, ep=zn[d] * 2 + core)
+        tell(barrier, ep=zn[d] * 2 + 1 - core)
+    tell(barrier, ep=z * 2 + 1 - core)
+    for c in l_w + l_x:
         c.start()
-    pl.semaphore_wait(barrier, 20)
-
+    pl.semaphore_wait(barrier, 9)
+
+    def tell_level(k):
+        for d in range(2):
+            tell(lv.at[k, d], ep=zn[d] * 2 + core)
+
+    def wait_level(k):
+        for d in range(2):
+            pl.semaphore_wait(lv.at[k, d], 1)
+
+    tell_level(0)
+
+    WIN = (wg, wu, wd)
     WB = (wgb, wub, wdb)
     HALF = (512, 512, 128)
-    xa = [[remote(WB[m].at[f], WB[m].at[f], xa_s.at[m, d], xa_r.at[m, d], fsdp=xn[d]) for d in range(2)] for m in range(3)]
+    xa = [[remote(WIN[m], WB[m].at[f], xa_s.at[m, d], xa_r.at[m, d], fsdp=xn[d]) for d in range(2)] for m in range(3)]
 
     def half_of(m, d, b):
         return WB[m].at[b, pl.ds(d * HALF[m], HALF[m]), :]
@@ -112,10 +130,11 @@
         for c in pair:
             c.start()
 
-    for m in (0, 1):
-        l_w[m].wait()
-        start(xa[m])
-
+    start(xa[0])
+    start(xa[1])
+
+    for c in l_r:
+        c.wait()
     r0, r1 = routes[0:1, :], routes[1:2, :]
     g0, g1 = logits[0:1, :], logits[1:2, :]
     gm = jnp.maximum(g0, g1)
@@ -158,9 +177,18 @@
         )
         for j in range(1, NJ)
     ]
-    for j in range(1, NJ):
-        za[j].start()
+    start(za[1:6])
+    wait_level(0)
+    tell_level(1)
+    start(za[6:10])
+    wait_level(1)
+    tell_level(2)
+    start(za[10:14])
+    wait_level(2)
+    start(za[14:])
     sb[t, 0:CAP, :] = outb[0:CAP, :]
+    for c in l_w:
+        c.wait()
 
     def add_block(dst, w, b, first):
         cols = pl.ds(pl.multiple_of(b * Q, Q), Q)
@@ -206,7 +234,6 @@
     rows_arrived(1)
     recv(xa[0])
     start(xf[0])
-    l_w[2].wait()
     start(xa[2])
     recv(ya[0])
     start(yf[0])
@@ -378,16 +405,16 @@
             back[0:CAP, :] = ret[0:CAP, :]
 
     slot_first(3)
+    slot_first(2)
     wide_grad((f + 2) % 4, ggb, store_bf16(x1g))
     start(x1[0])
-    slot_first(2)
+    slot_rest(3)
+    wide_grad((f + 2) % 4, gub, store_bf16(x1u))
+    start(x1[1])
+    slot_second(3)
     recv(x1[2])
     add_half(2, x2d, x1dr)
     start(x2[2])
-    wide_grad((f + 2) % 4, gub, store_bf16(x1u))
-    start(x1[1])
-    slot_rest(3)
-    slot_second(3)
     slot_first(1)
     slot_rest(2)
     slot_second(2)
@@ -395,32 +422,26 @@
     for j in range(1, NJ):
         zp[j].start()
     prr[0] = prt[0]
+    slot_rest(1)
+    slot_rest(0)
     wide_grad(up(f), ggb, store_bf16(x2g.at[0]))
     wide_grad(down(f), ggb, store_bf16(x2g.at[1]))
-    slot_rest(1)
+    slot_done(3)
     slot_second(1)
     recv(x1[0])
     add_half(0, x2g, x1gr)
     start(x2[0])
-    slot_done(3)
-    slot_rest(0)
-    slot_second(0)
     wide_grad(up(f), gub, store_bf16(x2u.at[0]))
     wide_grad(down(f), gub, store_bf16(x2u.at[1]))
+    slot_done(2)
+    slot_second(0)
+    down_grad(f, store_f32(gd_o))
+    wide_grad(f, ggb, store_f32(gg_o))
+    slot_done(1)
     recv(x1[1])
     add_half(1, x2u, x1ur)
     start(x2[1])
-    slot_done(2)
-    down_grad(f, store_f32(ownd))
-    wide_grad(f, ggb, store_f32(owng))
-    wide_grad(f, gub, store_f32(ownu))
-    slot_done(1)
-
-    outs = [
-        pltpu.make_async_copy(owng, gg_o, so.at[0]),
-        pltpu.make_async_copy(ownu, gu_o, so.at[1]),
-        pltpu.make_async_copy(ownd, gd_o, so.at[2]),
-    ]
+    wide_grad(f, gub, store_f32(gu_o))
 
     def finish(m, own, got):
         recv(x2[m])
@@ -431,9 +452,7 @@
             rows = pl.ds(pl.multiple_of(i * n, 64), n)
             own[rows, :] = own[rows, :] + got[0, rows, :].astype(F32) + got[1, rows, :].astype(F32)
 
-        outs[m].start()
-
-    finish(2, ownd, x2dr)
+    finish(2, gd_o, x2dr)
 
     for j in range(1, NJ):
         zp[j].wait_recv()
@@ -461,46 +480,50 @@
     for j in range(1, NJ):
         zb[j].wait_recv()
 
-    for i in range(2):
-        cols = pl.ds(512 * i, 512)
-        fin[t, :, cols] = dot_nn(qt[...], back[:, cols]).astype(BF16)
-    fa = [remote(fin.at[t], fin.at[t], fa_s.at[d], fa_r.at[d], tp=yn[d]) for d in range(2)]
-
-    def f_half(d):
-        return fin.at[tsrc[d], pl.ds(64 * d, 64), :]
-
-    ffw = [remote(f_half(d), f_half(d), ff_s.at[d], ff_r.at[d], tp=yn[d]) for d in range(2)]
-    start(fa)
+    def columns(b):
+        return pl.ds(pl.multiple_of(b * Q, Q), Q)
+
+    def part(b, h):
+        return ig_o.at[pl.ds(64 * h, 64), columns(b)]
+
+    fa = [[remote(part(t, h), part(t, h), fa_s.at[d, h], fa_r.at[d, h], tp=yn[d]) for h in range(2)] for d in range(2)]
+    ffw = [remote(part(tsrc[d], d), part(tsrc[d], d), ff_s.at[d], ff_r.at[d], tp=yn[d]) for d in range(2)]
+    for h in range(2):
+        ig_o[pl.ds(64 * h, 64), columns(t)] = dot_nn(qt[pl.ds(64 * h, 64), :], back[...]).astype(BF16)
+        fa[h][h].start()
+    fa[0][1].start()
+    fa[1][0].start()
     recv(cc)
     total = ((cr[0] + cr[1]) + cr[2]) + cr[3]
     chosen = total.astype(BF16).astype(F32)
     both = chosen[0:1, :] + chosen[1:2, :]
     pp = jnp.where(half8 == 0, p0, p1)
-    lg_o[...] = chosen - pp * both
-    finish(0, owng, x2gr)
-    o_own = pltpu.make_async_copy(fin.at[t], ig_o.at[:, pl.ds(tq, Q)], so.at[3])
-    o_own.start()
-    recv(fa)
-    start(ffw)
-    o_nb = []
+    lg_o[...] = (chosen - pp * both)[0:2, :]
+    finish(0, gg_o, x2gr)
     for d in range(2):
-        at = pl.multiple_of(tsrc[d] * Q, Q)
-        o_nb.append(pltpu.make_async_copy(fin.at[tsrc[d]], ig_o.at[:, pl.ds(at, Q)], so.at[4 + d]))
-    start(o_nb)
-    finish(1, ownu, x2ur)
+        fa[d][d].wait_recv()
+        ffw[d].start()
+    finish(1, gu_o, x2ur)
+    fa[0][1].wait_recv()
+    fa[1][0].wait_recv()
     recv(ffw)
-    opp = (t + 2) % 4
-    o_op = pltpu.make_async_copy(fin.at[opp], ig_o.at[:, pl.ds(pl.multiple_of(opp * Q, Q), Q)], so.at[6])
-    o_op.start()
 
     for group in (xa, xf, x1, x2, ya, yf, y1, y2):
         for pair in group:
             for c in pair:
                 c.wait_send()
-    for group in (za[1:], zb[1:], zp[1:], fa, ffw, cc):
+    for group in (za[1:], zb[1:], zp[1:], fa[0], fa[1], ffw, cc):
         for c in group:
             c.wait_send()
-    for c in outs + [o_own, o_op] + o_nb:
+
+
+def deliver(*refs):
+    n = len(refs) // 2
+    sems = refs[-1]
+    copies = [pltpu.make_async_copy(refs[i], refs[n + i], sems.at[i]) for i in range(n)]
+    for c in copies:
+        c.start()
+    for c in copies:
         c.wait()
 
 
@@ -513,7 +536,7 @@
         return pltpu.VMEM(shape, dtype)
 
     scratch = [
-        v(SLOTS, 4 * Q), v(4 * Q, SLOTS), v(4, Q, FFL), v(4, Q, FFL), v(4, FFL, Q),
+        v(2, TOK, dtype=I32), v(2, TOK, dtype=F32), v(SLOTS, 4 * Q), v(4 * Q, SLOTS), v(4, Q, FFL), v(4, Q, FFL), v(4, FFL, Q),
         v(TOK, Q), v(SLOTS, Q), v(4, SLOTS, Q),
         v(SLOTS, FFL, dtype=F32), v(SLOTS, FFL, dtype=F32), v(SLOTS, FFL, dtype=F32),
         v(SLOTS, FFL), v(FFL, SLOTS), v(SLOTS, FFL), v(SLOTS, FFL),
@@ -523,35 +546,46 @@
         v(SLOTS, Q, dtype=F32), v(SLOTS, Q), v(SLOTS, Q),
         v(Q, FFL), v(Q, FFL), v(FFL, Q), v(Q, FFL), v(Q, FFL), v(FFL, Q),
         v(2, Q, FFL), v(2, Q, FFL), v(2, FFL, Q), v(2, Q, FFL), v(2, Q, FFL), v(2, FFL, Q),
-        v(Q, FFL, dtype=F32), v(Q, FFL, dtype=F32), v(FFL, Q, dtype=F32),
-        v(4, TOK, Q), v(NCH, 8, 128, dtype=F32), v(NJ, 8, 128, dtype=F32),
+        v(NCH, 8, 128, dtype=F32), v(NJ, 8, 128, dtype=F32),
         v(8, 128, dtype=F32), v(4, 8, 128, dtype=F32),
-        dma((NJ,)), dma((3,)), dma((1,)), dma((7,)),
+        dma((NJ,)), dma((3,)), dma((3,)), pltpu.SemaphoreType.REGULAR((3, 2)),
         dma((3, 2)), dma((3, 2)), dma((3, 2)), dma((3, 2)), dma((3, 2)), dma((3, 2)), dma((3, 2)), dma((3, 2)),
         dma((4, 2)), dma((4, 2)), dma((4, 2)), dma((4, 2)), dma((4, 2)), dma((4, 2)), dma((4, 2)), dma((4, 2)),
         dma((NJ,)), dma((NJ,)), dma((NJ,)), dma((NJ,)), dma((NJ,)), dma((NJ,)),
-        dma((2,)), dma((2,)), dma((2,)), dma((2,)), dma((3,)), dma((3,)),
-    ]
-    ig, lg, gg, gu, gd = pl.pallas_call(
+        dma((2, 2)), dma((2, 2)), dma((2,)), dma((2,)), dma((3,)), dma((3,)),
+    ]
+    shapes = (
+        jax.ShapeDtypeStruct((TOK, 4 * Q), BF16),
+        jax.ShapeDtypeStruct((2, TOK), F32),
+        jax.ShapeDtypeStruct((Q, FFL), F32),
+        jax.ShapeDtypeStruct((Q, FFL), F32),
+        jax.ShapeDtypeStruct((FFL, Q), F32),
+    )
+    made = pl.pallas_call(
         kernel,
-        out_shape=(
-            jax.ShapeDtypeStruct((TOK, 4 * Q), BF16),
-            jax.ShapeDtypeStruct((8, 128), F32),
-            jax.ShapeDtypeStruct((Q, FFL), F32),
-            jax.ShapeDtypeStruct((Q, FFL), F32),
-            jax.ShapeDtypeStruct((FFL, Q), F32),
-        ),
-        in_specs=[vmem, vmem, hbm, hbm, hbm, hbm, hbm],
-        out_specs=(hbm, vmem, hbm, hbm, hbm),
+        out_shape=shapes,
+        in_specs=[hbm] * 7,
+        out_specs=(vmem,) * 5,
         scratch_shapes=scratch,
         compiler_params=pltpu.CompilerParams(
-            collective_id=0, has_side_effects=True, vmem_limit_bytes=60 * 1024 * 1024
+            collective_id=0, has_side_effects=True, vmem_limit_bytes=48 * 1024 * 1024
         ),
-    )(
-        routes.T, chosen_logits.T, out_grad,
-        routed_inputs.reshape(NJ, CAP, 4 * Q), w_gate[0], w_up[0], w_down[0],
-    )
-    return ig, lg[:2].T, gg[None], gu[None], gd[None]
+    )(*[
+        pltpu.with_memory_space_constraint(a, pltpu.HBM)
+        for a in (
+            routes.T, chosen_logits.T, out_grad,
+            routed_inputs.reshape(NJ, CAP, 4 * Q), w_gate[0], w_up[0], w_down[0],
+        )
+    ])
+    ig, lg, gg, gu, gd = pl.pallas_call(
+        deliver,
+        out_shape=shapes,
+        in_specs=[vmem] * 5,
+        out_specs=(hbm,) * 5,
+        scratch_shapes=[dma((5,))],
+        compiler_params=pltpu.CompilerParams(vmem_limit_bytes=4 * 1024 * 1024),
+    )(*made)
+    return ig, lg.T, gg[None], gu[None], gd[None]
 
 
 def solution(mesh):

time: 136 us -> 121 us (0.89)
  local copies, waits for them, and re-layouts: 7.89 us -> 0 us
  Pallas kernels: 127 us -> 120 us
    pallas_call x1 -> x2, Pallas kernels: 127 us -> 120 us  [the longest x1 118 us: on_device(): pl.pallas_call(kernel, out_shape=shapes, in_specs=[hbm] * 7, out_specs=(v...]
    unnamed x8 -> x0, local copies, waits for them, and re-layouts: 6.5 us -> none
    transpose x1 -> x0, local copies, waits for them, and re-layouts: 1.39 us -> none  [on_device(): return (ig, lg[:2].T, gg[None], gu[None], gd[None])]
where the time goes in v2:
time: 121 us
  Pallas kernels  120 us (99%)
    pallas_call x1, Pallas kernels, on_device(): pl.pallas_call(kernel, out_shape=shapes, in_specs=[hbm] * 7, out_specs=(v...  118 us

profile of v2, /device:TPU:1, one launch (start us, length us, event | category | flops | bytes accessed | tf_op | source)
XLA Modules:
  0.0 120.8 jit_solution(9911336905838796693)
XLA Ops:
  0.6 118.1 %shard_map.110 = (bf16[128,4096]{1,0:T(8,128)(2,1)S(1)}, f32[2,128]{1,0:T(2,128)S(1)}, f32[1024,256]{1,0:T(8,128)S(1)}, f32[1024,256]{1,0:T(8,128)S(1)}, f32[256,1024]{1,0:T(8,128)S(1)}) custom-call(s32[2,128]{1,0:T(2,128)} %bitcast.14, f32[2,128]{1,0:T(2,128)} %bitcast.15, bf16[128,4096]{1,0:T(8,128)(2,1)} %og.1, bf16[16,32,4096]{2,1,0:T(8,128)(2,1)} %bitcast.10, ...), custom_call_target="tpu_custom_call" | custom-call | tf_op jit(solution)/shard_map/pallas_call | solution.py:564
  118.8 2.1 %shard_map.111 = (bf16[128,4096]{1,0:T(8,128)(2,1)}, f32[2,128]{1,0:T(2,128)}, f32[1024,256]{1,0:T(8,128)}, f32[1024,256]{1,0:T(8,128)}, f32[256,1024]{1,0:T(8,128)}) custom-call(bf16[128,4096]{1,0:T(8,128)(2,1)S(1)} %get-tuple-element.15.refs_0_, f32[2,128]{1,0:T(2,128)S(1)} %get-tuple-element.16.refs_1_, f32[1024,256]{1,0:T(8,128)S(1)} %get-tuple-element.17.refs_2_, ...), custom_call_target="tpu_custom_call" | custom-call | tf_op jit(solution)/shard_map/pallas_call | solution.py:580

commit v3 on v2

--- a/solution.py
+++ b/solution.py
@@ -15,6 +15,7 @@
 CAP = 32
 TOK = 128
 NCH = 4
+NSUB = 8
 ROWS = 128
 SLOTS = 512
 Q = 1024
@@ -38,10 +39,8 @@
     y1s, y1r, y2s, y2r, sown, ret, back,
     x1g, x1u, x1d, x1gr, x1ur, x1dr, x2g, x2u, x2d, x2gr, x2ur, x2dr,
     prt, prr, cs, cr,
-    lx, lw, lo, lv,
-    xa_s, xa_r, xf_s, xf_r, x1_s, x1_rs, x2_s, x2_rs,
-    ya_s, ya_r, yf_s, yf_r, y1_s, y1_rs, y2_s, y2_rs,
-    za_s, za_r, zb_s, zb_r, zp_s, zp_r, fa_s, fa_r, ff_s, ff_r, c_s, c_r,
+    lx, lw, lo, lv, sent,
+    xa_r, xf_r, x1_rs, x2_rs, ya_r, yf_r, y1_rs, y2_rs, za_r, zb_r, zp_r, fa_r, ff_r, c_r,
 ):
     ep = lax.axis_index("ep")
     f = lax.axis_index("fsdp")
@@ -69,6 +68,12 @@
             src_ref=src, dst_ref=dst, send_sem=ss, recv_sem=rs, device_id=axis, device_id_type=MESH
         )
 
+    def arrived(ref, sem):
+        pltpu.make_async_copy(ref, ref, sem).wait()
+
+    def kib(n):
+        return xb.at[pl.ds(0, n // 8), :]
+
     tq = pl.multiple_of(t * Q, Q)
     l_og = pltpu.make_async_copy(og.at[:, pl.ds(tq, Q)], ogq, lo.at[0])
     l_r = [
@@ -83,7 +88,7 @@
         for m, (src, dst) in enumerate(((wg, wgb), (wu, wub), (wd, wdb)))
     ]
     l_x = [
-        pltpu.make_async_copy(x.at[source_of(j)], xb.at[pl.ds(CAP * j, CAP), :], lx.at[j])
+        pltpu.make_async_copy(x.at[source_of(j)], xb.at[pl.ds(CAP * j, CAP), :], lx.at[0])
         for j in range(NJ)
     ]
 
@@ -115,14 +120,14 @@
     WIN = (wg, wu, wd)
     WB = (wgb, wub, wdb)
     HALF = (512, 512, 128)
-    xa = [[remote(WIN[m], WB[m].at[f], xa_s.at[m, d], xa_r.at[m, d], fsdp=xn[d]) for d in range(2)] for m in range(3)]
+    xa = [[remote(WIN[m], WB[m].at[f], sent.at[0], xa_r.at[m], fsdp=xn[d]) for d in range(2)] for m in range(3)]
 
     def half_of(m, d, b):
         return WB[m].at[b, pl.ds(d * HALF[m], HALF[m]), :]
 
     fsrc = (down(f), up(f))
     xf = [
-        [remote(half_of(m, d, fsrc[d]), half_of(m, d, fsrc[d]), xf_s.at[m, d], xf_r.at[m, d], fsdp=xn[d]) for d in range(2)]
+        [remote(half_of(m, d, fsrc[d]), half_of(m, d, fsrc[d]), sent.at[1], xf_r.at[m], fsdp=xn[d]) for d in range(2)]
         for m in range(3)
     ]
 
@@ -173,7 +178,7 @@
     za = [None] + [
         remote(
             outb.at[pl.ds(CAP * j, CAP), :], sb.at[t, pl.ds(CAP * j, CAP), :],
-            za_s.at[j], za_r.at[j], ep=expert_of(j),
+            sent.at[2], za_r.at[j // 4], ep=expert_of(j),
         )
         for j in range(1, NJ)
     ]
@@ -202,13 +207,12 @@
             else:
                 dst[rows, :] += part
 
-    for c in l_x:
-        c.wait()
+    arrived(xb, lx.at[0])
     add_block(act_a, wgb, f, True)
 
     ya = [
         [
-            remote(sb.at[t, pl.ds(ROWS * c, ROWS), :], sb.at[t, pl.ds(ROWS * c, ROWS), :], ya_s.at[c, d], ya_r.at[c, d], tp=yn[d])
+            remote(sb.at[t, pl.ds(ROWS * c, ROWS), :], sb.at[t, pl.ds(ROWS * c, ROWS), :], sent.at[3], ya_r.at[c], tp=yn[d])
             for d in range(2)
         ]
         for c in range(NCH)
@@ -218,29 +222,25 @@
     def s_half(c, d):
         return sb.at[tsrc[d], pl.ds(ROWS * c + 64 * d, 64), :]
 
-    yf = [[remote(s_half(c, d), s_half(c, d), yf_s.at[c, d], yf_r.at[c, d], tp=yn[d]) for d in range(2)] for c in range(NCH)]
+    yf = [[remote(s_half(c, d), s_half(c, d), sent.at[4], yf_r.at[0], tp=yn[d]) for d in range(2)] for c in range(NCH)]
 
     def rows_arrived(c):
-        for j in range(max(1, 4 * c), 4 * c + 4):
-            za[j].wait_recv()
+        first = CAP if c == 0 else 0
+        arrived(sb.at[t, pl.ds(ROWS * c + first, ROWS - first), :], za_r.at[c])
         start(ya[c])
-
-    def recv(pair):
-        for c in pair:
-            c.wait_recv()
 
     rows_arrived(0)
     add_block(act_b, wub, f, True)
     rows_arrived(1)
-    recv(xa[0])
+    arrived(kib(1024), xa_r.at[0])
     start(xf[0])
     start(xa[2])
-    recv(ya[0])
+    arrived(kib(512), ya_r.at[0])
     start(yf[0])
     add_block(act_a, wgb, up(f), False)
     add_block(act_a, wgb, down(f), False)
     rows_arrived(2)
-    recv(ya[1])
+    arrived(kib(512), ya_r.at[1])
     start(yf[1])
 
     def transpose_x(lo_, hi_):
@@ -249,18 +249,18 @@
             at = pl.ds(pl.multiple_of(i * 256, 256), 256)
             xt[at, :] = xb[:, at].T
 
-    recv(xa[1])
+    arrived(kib(1024), xa_r.at[1])
     start(xf[1])
     add_block(act_b, wub, up(f), False)
     add_block(act_b, wub, down(f), False)
     rows_arrived(3)
-    recv(ya[2])
+    arrived(kib(512), ya_r.at[2])
     start(yf[2])
     transpose_x(0, 8)
-    recv(xf[0])
+    arrived(kib(512), xf_r.at[0])
     add_block(act_a, wgb, (f + 2) % 4, False)
     transpose_x(8, 16)
-    recv(ya[3])
+    arrived(kib(512), ya_r.at[3])
     start(yf[3])
 
     def add_hidden(b, first):
@@ -273,14 +273,13 @@
             else:
                 hg[rows, :] += part
 
-    recv(xa[2])
+    arrived(kib(1024), xa_r.at[2])
     start(xf[2])
-    for c in range(NCH):
-        recv(yf[c])
+    arrived(kib(1024), yf_r.at[0])
     for k in (0, 1, 3):
         add_hidden((f + k) % 4, k == 0)
     qt[...] = qs[...].T
-    recv(xf[1])
+    arrived(kib(512), xf_r.at[1])
     add_block(act_b, wub, (f + 2) % 4, False)
 
     @pl.loop(0, 8)
@@ -298,12 +297,12 @@
     def x1_pair(m, s, r):
         h = HALF[m]
         return [
-            remote(s.at[pl.ds(h * d, h), :], r.at[pl.ds(h * d, h), :], x1_s.at[m, d], x1_rs.at[m, d], fsdp=xn[d])
+            remote(s.at[pl.ds(h * d, h), :], r.at[pl.ds(h * d, h), :], sent.at[5], x1_rs.at[m], fsdp=xn[d])
             for d in range(2)
         ]
 
     def x2_pair(m, s, r):
-        return [remote(s.at[d], r.at[d], x2_s.at[m, d], x2_rs.at[m, d], fsdp=xn[d]) for d in range(2)]
+        return [remote(s.at[d], r.at[d], sent.at[6], x2_rs.at[m], fsdp=xn[d]) for d in range(2)]
 
     x1 = [x1_pair(0, x1g, x1gr), x1_pair(1, x1u, x1ur), x1_pair(2, x1d, x1dr)]
     x2 = [x2_pair(0, x2g, x2gr), x2_pair(1, x2u, x2ur), x2_pair(2, x2d, x2dr)]
@@ -348,7 +347,7 @@
     down_grad(up(f), store_bf16(x2d.at[0]))
     down_grad(down(f), store_bf16(x2d.at[1]))
 
-    recv(xf[2])
+    arrived(kib(512), xf_r.at[2])
     add_hidden((f + 2) % 4, False)
 
     for c in range(NCH):
@@ -361,47 +360,55 @@
 
     y1 = [
         [
-            remote(y1s.at[c, pl.ds(64 * d, 64), :], y1r.at[c, pl.ds(64 * d, 64), :], y1_s.at[c, d], y1_rs.at[c, d], tp=yn[d])
+            remote(y1s.at[pl.ds(64 * i + 32 * d, 32), :], y1r.at[pl.ds(64 * i + 32 * d, 32), :], sent.at[7], y1_rs.at[i], tp=yn[d])
             for d in range(2)
         ]
-        for c in range(NCH)
-    ]
-    y2 = [[remote(y2s.at[c, d], y2r.at[c, d], y2_s.at[c, d], y2_rs.at[c, d], tp=yn[d]) for d in range(2)] for c in range(NCH)]
+        for i in range(NSUB)
+    ]
+    y2 = [
+        [
+            remote(y2s.at[d, pl.ds(64 * i, 64), :], y2r.at[d, pl.ds(64 * i, 64), :], sent.at[8], y2_rs.at[i], tp=yn[d])
+            for d in range(2)
+        ]
+        for i in range(NSUB)
+    ]
 
     def slot_block(c, b):
         rows = pl.ds(ROWS * c, ROWS)
         return dot_nt(ggb[rows, :], wgb[b]) + dot_nt(gub[rows, :], wub[b])
 
     def slot_first(c):
-        y1s[c] = slot_block(c, (t + 2) % 4).astype(BF16)
-        start(y1[c])
+        y1s[pl.ds(ROWS * c, ROWS), :] = slot_block(c, (t + 2) % 4).astype(BF16)
+        start(y1[2 * c + 1])
+        start(y1[2 * c])
 
     def slot_rest(c):
-        y2s[c, 0] = slot_block(c, up(t)).astype(BF16)
-        y2s[c, 1] = slot_block(c, down(t)).astype(BF16)
-        sown[pl.ds(ROWS * c, ROWS), :] = slot_block(c, t)
-
-    def slot_second(c):
-        recv(y1[c])
+        rows = pl.ds(ROWS * c, ROWS)
+        y2s[0, rows, :] = slot_block(c, up(t)).astype(BF16)
+        y2s[1, rows, :] = slot_block(c, down(t)).astype(BF16)
+        sown[rows, :] = slot_block(c, t)
+
+    def slot_second(i):
+        arrived(kib(128), y1_rs.at[i])
         for d in range(2):
-            rows = pl.ds(64 * d, 64)
-            y2s[c, d, rows, :] = (y2s[c, d, rows, :].astype(F32) + y1r[c, rows, :].astype(F32)).astype(BF16)
-        start(y2[c])
+            rows = pl.ds(64 * i + 32 * d, 32)
+            y2s[d, rows, :] = (y2s[d, rows, :].astype(F32) + y1r[rows, :].astype(F32)).astype(BF16)
+        start(y2[i])
 
     zb = [None] + [
-        remote(ret.at[pl.ds(CAP * j, CAP), :], back.at[pl.ds(CAP * j, CAP), :], zb_s.at[j], zb_r.at[j], ep=source_of(j))
+        remote(ret.at[pl.ds(CAP * j, CAP), :], back.at[pl.ds(CAP * j, CAP), :], sent.at[9], zb_r.at[0], ep=source_of(j))
         for j in range(1, NJ)
     ]
-    zp = [None] + [remote(prt.at[j // 4], prr.at[j], zp_s.at[j], zp_r.at[j], ep=source_of(j)) for j in range(1, NJ)]
-
-    def slot_done(c):
-        recv(y2[c])
-        rows = pl.ds(ROWS * c, ROWS)
-        total = sown[rows, :] + y2r[c, 0].astype(F32) + y2r[c, 1].astype(F32)
+    zp = [None] + [remote(prt.at[j // 4], prr.at[j], sent.at[10], zp_r.at[0], ep=source_of(j)) for j in range(1, NJ)]
+
+    def slot_done(i):
+        arrived(kib(256), y2_rs.at[i])
+        rows = pl.ds(64 * i, 64)
+        total = sown[rows, :] + y2r[0, rows, :].astype(F32) + y2r[1, rows, :].astype(F32)
         ret[rows, :] = total.astype(BF16)
-        for j in range(max(1, 4 * c), 4 * c + 4):
+        for j in range(max(1, 2 * i), 2 * i + 2):
             zb[j].start()
-        if c == 0:
+        if i == 0:
             back[0:CAP, :] = ret[0:CAP, :]
 
     slot_first(3)
@@ -409,42 +416,50 @@
     wide_grad((f + 2) % 4, ggb, store_bf16(x1g))
     start(x1[0])
     slot_rest(3)
+    slot_second(7)
     wide_grad((f + 2) % 4, gub, store_bf16(x1u))
     start(x1[1])
-    slot_second(3)
-    recv(x1[2])
+    slot_second(6)
+    arrived(kib(512), x1_rs.at[2])
     add_half(2, x2d, x1dr)
     start(x2[2])
     slot_first(1)
     slot_rest(2)
-    slot_second(2)
+    slot_second(5)
+    slot_second(4)
     slot_first(0)
     for j in range(1, NJ):
         zp[j].start()
     prr[0] = prt[0]
     slot_rest(1)
+    slot_done(7)
     slot_rest(0)
+    slot_done(6)
     wide_grad(up(f), ggb, store_bf16(x2g.at[0]))
     wide_grad(down(f), ggb, store_bf16(x2g.at[1]))
-    slot_done(3)
-    slot_second(1)
-    recv(x1[0])
+    slot_second(3)
+    slot_second(2)
+    arrived(kib(512), x1_rs.at[0])
     add_half(0, x2g, x1gr)
     start(x2[0])
     wide_grad(up(f), gub, store_bf16(x2u.at[0]))
     wide_grad(down(f), gub, store_bf16(x2u.at[1]))
-    slot_done(2)
+    slot_done(5)
+    slot_done(4)
+    slot_second(1)
     slot_second(0)
     down_grad(f, store_f32(gd_o))
+    slot_done(3)
     wide_grad(f, ggb, store_f32(gg_o))
-    slot_done(1)
-    recv(x1[1])
+    slot_done(2)
+    arrived(kib(512), x1_rs.at[1])
     add_half(1, x2u, x1ur)
     start(x2[1])
+    slot_done(1)
     wide_grad(f, gub, store_f32(gu_o))
 
     def finish(m, own, got):
-        recv(x2[m])
+        arrived(kib(1024), x2_rs.at[m])
         n = own.shape[0] // 4
 
         @pl.loop(0, 4)
@@ -454,8 +469,7 @@
 
     finish(2, gd_o, x2dr)
 
-    for j in range(1, NJ):
-        zp[j].wait_recv()
+    arrived(prr.at[pl.ds(1, NJ - 1)], zp_r.at[0])
     lane = lax.broadcasted_iota(I32, (8, 128), 1) // CAP
     ch = [jnp.zeros((8, TOK), F32), jnp.zeros((8, TOK), F32)]
     for c in range(NCH):
@@ -470,15 +484,14 @@
     half8 = lax.broadcasted_iota(I32, (8, TOK), 0)
     cs[...] = jnp.where(half8 == 0, ch[0], ch[1])
     cc = [
-        remote(cs, cr.at[t], c_s.at[k - 1], c_r.at[k - 1], tp=(t + k) % 4) for k in (1, 2, 3)
+        remote(cs, cr.at[t], sent.at[11], c_r.at[0], tp=(t + k) % 4) for k in (1, 2, 3)
     ]
     start(cc)
     cr[t] = cs[...]
 
     slot_done(0)
 
-    for j in range(1, NJ):
-        zb[j].wait_recv()
+    arrived(back.at[pl.ds(CAP, SLOTS - CAP), :], zb_r.at[0])
 
     def columns(b):
         return pl.ds(pl.multiple_of(b * Q, Q), Q)
@@ -486,14 +499,14 @@
     def part(b, h):
         return ig_o.at[pl.ds(64 * h, 64), columns(b)]
 
-    fa = [[remote(part(t, h), part(t, h), fa_s.at[d, h], fa_r.at[d, h], tp=yn[d]) for h in range(2)] for d in range(2)]
-    ffw = [remote(part(tsrc[d], d), part(tsrc[d], d), ff_s.at[d], ff_r.at[d], tp=yn[d]) for d in range(2)]
+    fa = [[remote(part(t, h), part(t, h), sent.at[12], fa_r.at[d, h], tp=yn[d]) for h in range(2)] for d in range(2)]
+    ffw = [remote(part(tsrc[d], d), part(tsrc[d], d), sent.at[13], ff_r.at[0], tp=yn[d]) for d in range(2)]
     for h in range(2):
         ig_o[pl.ds(64 * h, 64), columns(t)] = dot_nn(qt[pl.ds(64 * h, 64), :], back[...]).astype(BF16)
         fa[h][h].start()
     fa[0][1].start()
     fa[1][0].start()
-    recv(cc)
+    arrived(cr.at[pl.ds(0, 3)], c_r.at[0])
     total = ((cr[0] + cr[1]) + cr[2]) + cr[3]
     chosen = total.astype(BF16).astype(F32)
     both = chosen[0:1, :] + chosen[1:2, :]
@@ -506,15 +519,14 @@
     finish(1, gu_o, x2ur)
     fa[0][1].wait_recv()
     fa[1][0].wait_recv()
-    recv(ffw)
-
-    for group in (xa, xf, x1, x2, ya, yf, y1, y2):
-        for pair in group:
-            for c in pair:
-                c.wait_send()
-    for group in (za[1:], zb[1:], zp[1:], fa[0], fa[1], ffw, cc):
-        for c in group:
-            c.wait_send()
+    arrived(kib(256), ff_r.at[0])
+
+    for i, n in ((0, 3072), (1, 1536), (3, 2048), (4, 1024), (5, 1536), (6, 3072), (7, 1024), (8, 2048), (12, 512), (13, 256)):
+        arrived(kib(n), sent.at[i])
+    arrived(outb.at[pl.ds(CAP, SLOTS - CAP), :], sent.at[2])
+    arrived(ret.at[pl.ds(CAP, SLOTS - CAP), :], sent.at[9])
+    arrived(prr.at[pl.ds(1, NJ - 1)], sent.at[10])
+    arrived(cr.at[pl.ds(0, 3)], sent.at[11])
 
 
 def deliver(*refs):
@@ -542,17 +554,15 @@
         v(SLOTS, FFL), v(FFL, SLOTS), v(SLOTS, FFL), v(SLOTS, FFL),
         v(SLOTS, TOK), v(TOK, SLOTS), v(2, SLOTS, TOK, dtype=F32), v(SLOTS, TOK, dtype=F32),
         v(NJ, TOK, dtype=F32), v(NJ, TOK, dtype=F32), v(NJ, TOK, dtype=F32),
-        v(NCH, ROWS, Q), v(NCH, ROWS, Q), v(NCH, 2, ROWS, Q), v(NCH, 2, ROWS, Q),
+        v(SLOTS, Q), v(SLOTS, Q), v(2, SLOTS, Q), v(2, SLOTS, Q),
         v(SLOTS, Q, dtype=F32), v(SLOTS, Q), v(SLOTS, Q),
         v(Q, FFL), v(Q, FFL), v(FFL, Q), v(Q, FFL), v(Q, FFL), v(FFL, Q),
         v(2, Q, FFL), v(2, Q, FFL), v(2, FFL, Q), v(2, Q, FFL), v(2, Q, FFL), v(2, FFL, Q),
         v(NCH, 8, 128, dtype=F32), v(NJ, 8, 128, dtype=F32),
         v(8, 128, dtype=F32), v(4, 8, 128, dtype=F32),
-        dma((NJ,)), dma((3,)), dma((3,)), pltpu.SemaphoreType.REGULAR((3, 2)),
-        dma((3, 2)), dma((3, 2)), dma((3, 2)), dma((3, 2)), dma((3, 2)), dma((3, 2)), dma((3, 2)), dma((3, 2)),
-        dma((4, 2)), dma((4, 2)), dma((4, 2)), dma((4, 2)), dma((4, 2)), dma((4, 2)), dma((4, 2)), dma((4, 2)),
-        dma((NJ,)), dma((NJ,)), dma((NJ,)), dma((NJ,)), dma((NJ,)), dma((NJ,)),
-        dma((2, 2)), dma((2, 2)), dma((2,)), dma((2,)), dma((3,)), dma((3,)),
+        dma((1,)), dma((3,)), dma((3,)), pltpu.SemaphoreType.REGULAR((3, 2)), dma((14,)),
+        dma((3,)), dma((3,)), dma((3,)), dma((3,)), dma((NCH,)), dma((1,)), dma((NSUB,)), dma((NSUB,)),
+        dma((NCH,)), dma((1,)), dma((1,)), dma((2, 2)), dma((1,)), dma((1,)),
     ]
     shapes = (
         jax.ShapeDtypeStruct((TOK, 4 * Q), BF16),

time: 121 us -> 117 us (0.967)
  Pallas kernels: 120 us -> 116 us
    pallas_call x1, Pallas kernels: 118 us -> 114 us  [on_device(): pl.pallas_call(kernel, out_shape=shapes, in_specs=[hbm] * 7, out_specs=(v...]
where the time goes in v3:
time: 117 us; the launch traced here: 116 us
  Pallas kernels  116 us (99%)
    pallas_call x1, Pallas kernels, on_device(): pl.pallas_call(kernel, out_shape=shapes, in_specs=[hbm] * 7, out_specs=(v...  114 us

profile of v3, /device:TPU:1, one launch (start us, length us, event | category | flops | bytes accessed | tf_op | source)
XLA Modules:
  0.0 116.5 jit_solution(881808681058430976)
XLA Ops:
  0.6 113.8 %shard_map.110 = (bf16[128,4096]{1,0:T(8,128)(2,1)S(1)}, f32[2,128]{1,0:T(2,128)S(1)}, f32[1024,256]{1,0:T(8,128)S(1)}, f32[1024,256]{1,0:T(8,128)S(1)}, f32[256,1024]{1,0:T(8,128)S(1)}) custom-call(s32[2,128]{1,0:T(2,128)} %bitcast.14, f32[2,128]{1,0:T(2,128)} %bitcast.15, bf16[128,4096]{1,0:T(8,128)(2,1)} %og.1, bf16[16,32,4096]{2,1,0:T(8,128)(2,1)} %bitcast.10, ...), custom_call_target="tpu_custom_call" | custom-call | tf_op jit(solution)/shard_map/pallas_call | solution.py:574
  114.4 2.1 %shard_map.111 = (bf16[128,4096]{1,0:T(8,128)(2,1)}, f32[2,128]{1,0:T(2,128)}, f32[1024,256]{1,0:T(8,128)}, f32[1024,256]{1,0:T(8,128)}, f32[256,1024]{1,0:T(8,128)}) custom-call(bf16[128,4096]{1,0:T(8,128)(2,1)S(1)} %get-tuple-element.15.refs_0_, f32[2,128]{1,0:T(2,128)S(1)} %get-tuple-element.16.refs_1_, f32[1024,256]{1,0:T(8,128)S(1)} %get-tuple-element.17.refs_2_, ...), custom_call_target="tpu_custom_call" | custom-call | tf_op jit(solution)/shard_map/pallas_call | solution.py:590
